TPU v7x, 32 devices: a whole 2x2x4 slice. The times are simulated.
32 devices in a mesh: grp: 4 (over x, core), lat: 8 (over z, y).
Axes of the slice: x: 2, y: 2, z: 4, core: 2. Of those that a mesh axis runs over, the one named last changes fastest.
Arguments:
- grid_state: bfloat16 [16, 192, 384, 128], P('grp', 'lat'), may hold values from -6 to 6
- noise_field: bfloat16 [16, 192, 384, 128], P('grp', 'lat'), may hold values from -6 to 6
- legendre: bfloat16 [192, 128, 128], P('lat'), may hold values from -0.4375 to 0.4375
- diffusion: float32 [128], replicated, may hold values from 0.1 to 10
- input_weight: bfloat16 [128, 256], replicated, may hold values from -0.5 to 0.5
- noise_weight: bfloat16 [128, 256], replicated, may hold values from -0.5 to 0.5
- input_bias: float32 [256], replicated, may hold values from -4 to 4
- middle_weight: bfloat16 [256, 256], replicated, may hold values from -0.375 to 0.375
- output_weight: bfloat16 [256, 128], replicated, may hold values from -0.375 to 0.375
Outputs:
- new_state: bfloat16 [16, 192, 384, 128], P('grp', 'lat')
- ens_mean: float32 [192, 384, 128], P('lat')
- ens_var: float32 [192, 384, 128], P('lat')
All inputs are finite; a program needn't handle non-finite values.
Results may differ from a plain program's by a relative error of at most 0.012.
Values may be sent and summed in bfloat16 or wider, within the bound.
A program may use at most 192 MiB of HBM per device.

v0:
```python
import math

import jax
import jax.numpy as jnp
from jax import lax
from jax.sharding import PartitionSpec as P


def wave_table(lon_count, wave_count):
    lon_ids = jnp.arange(lon_count, dtype=jnp.int32)[:, None]
    wave_ids = jnp.arange(wave_count, dtype=jnp.int32)[None, :]
    phase = (lon_ids * wave_ids % lon_count).astype(jnp.float32) * (2.0 * math.pi / lon_count)
    factor = math.sqrt(2.0 / lon_count)
    joined = jnp.concatenate([jnp.cos(phase), -jnp.sin(phase)], axis=1) * factor
    return joined.astype(jnp.bfloat16)


def damping_filter(diffusion, wave_count):
    degree = jnp.arange(wave_count, dtype=jnp.int32).astype(jnp.float32)
    ratio = degree * (degree + 1.0) / float((wave_count - 1) * wave_count)
    return 1.0 / (1.0 + diffusion[None, :] * (ratio * ratio)[:, None])


def per_device(
    grid_state,
    noise_field,
    legendre,
    diffusion,
    input_weight,
    noise_weight,
    input_bias,
    middle_weight,
    output_weight,
):
    members, lat_rows, lon_count, channels = grid_state.shape
    wave_count = legendre.shape[1]
    local_waves = wave_count // lax.axis_size("lat")
    transform = wave_table(lon_count, wave_count)
    fourier = jnp.einsum(
        "blxc,xk->blkc", grid_state, transform, preferred_element_type=jnp.float32
    ).astype(jnp.bfloat16)
    fourier = fourier.reshape(members, lat_rows, 2, wave_count, channels)
    basis_band = lax.all_to_all(legendre, "lat", split_axis=1, concat_axis=0, tiled=True)
    zonal_ids = lax.axis_index("lat") * local_waves + jnp.arange(local_waves, dtype=jnp.int32)
    total_ids = jnp.arange(wave_count, dtype=jnp.int32)
    triangle = (total_ids[None, :] >= zonal_ids[:, None]).astype(jnp.float32)
    damping = damping_filter(diffusion, wave_count)
    spectrum = jnp.einsum(
        "lmn,blrmc->brmnc",
        basis_band,
        lax.all_to_all(fourier, "lat", split_axis=3, concat_axis=1, tiled=True),
        preferred_element_type=jnp.float32,
    )
    spectrum = spectrum * triangle[None, None, :, :, None]
    filtered = (spectrum * damping[None, None, None, :, :]).astype(jnp.bfloat16)
    banded_grid = jnp.einsum(
        "lmn,brmnc->blrmc", basis_band, filtered, preferred_element_type=jnp.float32
    ).astype(jnp.bfloat16)
    grid_fourier = lax.all_to_all(banded_grid, "lat", split_axis=1, concat_axis=3, tiled=True)
    grid_fourier = grid_fourier.reshape(members, lat_rows, 2 * wave_count, channels)
    smoothed = jnp.einsum(
        "bljc,xj->blxc", grid_fourier, transform, preferred_element_type=jnp.float32
    )
    flat_fields = smoothed.reshape(-1, channels)
    smoothed_in = flat_fields.astype(jnp.bfloat16)
    pre_act = jnp.dot(smoothed_in, input_weight, preferred_element_type=jnp.float32)
    pre_act = pre_act + jnp.dot(
        noise_field.reshape(-1, noise_field.shape[3]),
        noise_weight,
        preferred_element_type=jnp.float32,
    )
    hidden_one = jax.nn.silu(pre_act + input_bias).astype(jnp.bfloat16)
    hidden_two = jax.nn.silu(
        jnp.dot(hidden_one, middle_weight, preferred_element_type=jnp.float32)
    ).astype(jnp.bfloat16)
    tendency = jnp.dot(hidden_two, output_weight, preferred_element_type=jnp.float32)
    new_state = (flat_fields + tendency).astype(jnp.bfloat16).reshape(grid_state.shape)
    member_values = new_state.astype(jnp.float32)
    ensemble = members * lax.axis_size("grp")
    summed = lax.psum(jnp.sum(member_values, axis=0).astype(jnp.bfloat16), "grp").astype(
        jnp.float32
    )
    ens_mean = summed / ensemble
    spread = lax.psum(
        jnp.sum(jnp.square(member_values - ens_mean), axis=0).astype(jnp.bfloat16), "grp"
    ).astype(jnp.float32)
    ens_var = spread / (ensemble - 1)
    return (new_state, ens_mean, ens_var)


def solution(mesh):
    in_specs = (
        P("grp", "lat", None, None),
        P("grp", "lat", None, None),
        P("lat", None, None),
        P(),
        P(),
        P(),
        P(),
        P(),
        P(),
    )
    out_specs = (P("grp", "lat", None, None), P("lat", None, None), P("lat", None, None))
    return jax.shard_map(
        per_device, mesh=mesh, in_specs=in_specs, out_specs=out_specs, check_vma=False
    )
```

profile of v0, /device:TPU:0, one launch (start us, length us, event | category | flops | bytes accessed | tf_op | source)
XLA Modules:
  0.0 592.6 jit_solution(8928592732857764437)
XLA Ops:
  7.2 0.0 copy-start
  7.2 2.6 copy.27
  9.7 7.3 %all-to-all-start.1 = ((bf16[24,128,128]{2,0,1:T(8,128)(2,1)}), bf16[24,128,128]{2,0,1:T(8,128)(2,1)S(1)}, u32[]{:S(2)}, u32[]{:S(2)}) async-start(bf16[24,128,128]{2,0,1:T(8,128)(2,1)} %copy.27), calls=%async_computation.1 | async-start | bytes 1572864 | tf_op jit(solution)/shard_map/all_to_all | solution.py:43
  17.0 0.8 sine_negate_fusion
  17.9 7.4 %convolution_convert_fusion = bf16[256,4,24,128]{3,0,2,1:T(8,128)(2,1)S(1)} fusion(bf16[4,24,384,128]{3,2,1,0:T(8,128)(2,1)} %param.9, f32[384,128]{0,1:T(8,128)S(1)} %get-tuple-element.3, f32[384,128]{0,1:T(8,128)S(1)} %get-tuple-element.4), kind=kOutput, calls=%fused_computation.19 | convolution fusion | flops 2419359744 | bytes 16121856 | tf_op jit(solution)/shard_map/blxc,xk->blkc/dot_general | solution.py:39
  25.2 20.3 %copy.24 = bf16[4,24,2,128,128]{4,2,1,0,3:T(2,128)(2,1)} copy(bf16[4,24,2,128,128]{4,3,2,1,0:T(8,128)(2,1)S(1)} %bitcast.52) | data formatting | bytes 12582912 | tf_op jit(solution)/shard_map/reshape | solution.py:42
  45.6 0.0 copy-start.4
  45.6 0.0 all-to-all-done.1
  45.6 6.1 %all-to-all-start = ((bf16[4,24,2,128,128]{4,2,1,0,3:T(2,128)(2,1)}), bf16[4,24,2,128,128]{4,2,1,0,3:T(2,128)(2,1)}, u32[]{:S(2)}, u32[]{:S(2)}) async-start(bf16[4,24,2,128,128]{4,2,1,0,3:T(2,128)(2,1)} %copy.24), calls=%async_computation | async-start | bytes 12582912 | tf_op jit(solution)/shard_map/all_to_all | solution.py:51
  51.7 0.2 all-reduce.3.cloned.1.call-start
  51.9 0.1 fusion.27
  52.0 0.0 copy-done.4
  52.0 0.1 add_divide_fusion
  52.1 0.1 copy.28
  52.2 137.1 %all-to-all-done = bf16[4,24,2,128,128]{4,2,1,0,3:T(2,128)(2,1)} async-done(((bf16[4,24,2,128,128]{4,2,1,0,3:T(2,128)(2,1)}), bf16[4,24,2,128,128]{4,2,1,0,3:T(2,128)(2,1)}, u32[]{:S(2)}, u32[]{:S(2)}) %all-to-all-start) | async-done | bytes 6291488 | tf_op jit(solution)/shard_map/all_to_all | solution.py:51
  189.4 10.1 %copy.25 = bf16[4,24,2,128,128]{4,3,2,1,0:T(8,128)(2,1)S(1)} copy(bf16[4,24,2,128,128]{4,2,1,0,3:T(2,128)(2,1)} %all-to-all-done) | data formatting | bytes 12582912 | tf_op jit(solution)/shard_map/all_to_all | solution.py:51
  199.4 4.4 copy.26
  203.8 8.6 %convert_bitcast_fusion = bf16[4,192,2,16,128]{4,1,2,0,3:T(8,128)(2,1)} fusion(bf16[192,16,128,1,1]{2,0,4,3,1:T(8,128)(2,1)S(1)} %bitcast.61, f32[128,128]{0,1:T(8,128)S(1)} %add_divide_fusion, f32[16,128]{1,0:T(8,128)S(1)} %fusion.27, bf16[4,192,2,16,128]{4,3,2,1,0:T(8,128)(2,1)} %bitcast.59), kind=kOutput, calls=%fused_computation.13 | convolution fusion | flops 1620049920 | bytes 13443072 | tf_op jit(solution)/shard_map/lmn,brmnc->blrmc/dot_general | solution.py:56
  212.4 9.5 %copy.31 = bf16[4,192,2,16,128]{4,2,0,3,1:T(2,128)(2,1)S(1)} copy(bf16[4,192,2,16,128]{4,1,2,0,3:T(8,128)(2,1)} %convert_bitcast_fusion) | data formatting | bytes 12582912 | tf_op jit(solution)/shard_map/convert_element_type | solution.py:58
  221.9 141.7 %all_to_all.51 = bf16[4,192,2,16,128]{4,2,0,3,1:T(2,128)(2,1)S(1)} all-to-all(bf16[4,192,2,16,128]{4,2,0,3,1:T(2,128)(2,1)S(1)} %copy.31), channel_id=1, replica_groups=mesh['grp'=4,'lat'=8] {'lat'}, dimensions={1} | all-to-all | bytes 12582912 | tf_op jit(solution)/shard_map/all_to_all | solution.py:59
  363.5 1.8 copy.32
  365.4 2.7 fusion.25
  368.0 0.0 copy-start.2
  368.1 6.4 %copy-done.2 = f32[384,4,24,128]{3,0,2,1:T(8,128)} copy-done((f32[384,4,24,128]{3,0,2,1:T(8,128)}, f32[384,4,24,128]{3,0,2,1:T(8,128)S(1)}, u32[]{:S(2)}) %copy-start.2) | copy-done | bytes 18874392
  374.5 0.0 copy-start.3
  374.5 4.3 bitcast_convert_fusion
  378.8 0.0 copy-done.3
  378.8 0.0 copy-start.5
  378.8 0.0 copy-start.7
  378.8 16.9 %fusion.36 = f32[36864,256]{1,0:T(8,128)} fusion(bf16[36864,128]{1,0:T(8,128)(2,1)} %bitcast_convert_fusion, bf16[128,256]{1,0:T(8,128)(2,1)S(1)} %copy-done.3), kind=kOutput, calls=%fused_computation.46 | convolution fusion | flops 2415919104 | bytes 47251456 | tf_op jit(solution)/shard_map/dot_general | solution.py:66
  395.7 0.0 copy-done
  395.7 0.0 copy-done.5
  395.8 0.0 copy-done.7
  395.8 0.0 copy-start.6
  395.8 27.9 %fusion.2 = f32[36864,256]{1,0:T(8,128)} fusion(bf16[256,256]{1,0:T(8,128)(2,1)S(1)} %copy-done, f32[36864,256]{1,0:T(8,128)} %fusion.36, bf16[36864,128]{1,0:T(8,128)(2,1)} %bitcast.62, bf16[128,256]{1,0:T(8,128)(2,1)S(1)} %copy-done.5, f32[256]{0:T(256)S(1)} %copy-done.7), kind=kOutput, calls=%fused_computation.8 | convolution fusion | flops 7313817600 | bytes 85132288 | tf_op jit(solution)/shard_map/dot_general | solution.py:74
  423.6 0.0 copy-done.6
  423.6 24.7 %fusion.1 = bf16[36864,128]{1,0:T(8,128)(2,1)} fusion(f32[36864,128]{1,0:T(8,128)} %bitcast.51, bf16[256,128]{1,0:T(8,128)(2,1)S(1)} %copy-done.6, f32[36864,256]{1,0:T(8,128)} %fusion.2), kind=kOutput, calls=%fused_computation.3 | convolution fusion | flops 2472542208 | bytes 66125824 | tf_op jit(solution)/shard_map/dot_general | solution.py:76
  448.4 7.6 %reduce_sum.21 = bf16[24,384,128]{2,1,0:T(8,128)(2,1)} reduce(bf16[4,24,384,128]{3,2,1,0:T(8,128)(2,1)} %bitcast.53, bf16[]{:T(256)} %constant.37.clone.1), dimensions={0}, to_apply=%region_0.1 | reduce | flops 3538944 | bytes 11796482 | tf_op jit(solution)/shard_map/reduce_sum | solution.py:80
  455.9 0.0 all-reduce.3.cloned.1.call-update
  455.9 0.0 all-reduce.5.cloned.1.call-start
  456.0 54.8 %all-reduce.3.cloned.1.call-done = bf16[24,384,128]{2,1,0:T(8,128)(2,1)} async-done(((bf16[24,384,128]{2,1,0:T(8,128)(2,1)}), bf16[24,384,128]{2,1,0:T(8,128)(2,1)}) %all-reduce.3.cloned.1.call-update) | async-done | bytes 2359312 | tf_op jit(solution)/shard_map/psum | solution.py:80
  510.8 0.0 copy-start.1
  510.8 4.4 convert_multiply_fusion.1
  515.2 9.8 %multiply_reduce_fusion = bf16[24,384,128]{2,1,0:T(8,128)(2,1)} fusion(bf16[4,24,384,128]{3,2,1,0:T(8,128)(2,1)} %bitcast.54, f32[24,384,128]{2,1,0:T(8,128)} %convert_multiply_fusion.1), kind=kLoop, calls=%fused_computation.7 | loop fusion | flops 17694720 | bytes 16515072 | tf_op jit(solution)/shard_map/reduce_sum | solution.py:85
  525.0 0.0 all-reduce.5.cloned.1.call-update
  525.0 55.9 %all-reduce.5.cloned.1.call-done = bf16[24,384,128]{2,1,0:T(8,128)(2,1)} async-done(((bf16[24,384,128]{2,1,0:T(8,128)(2,1)}), bf16[24,384,128]{2,1,0:T(8,128)(2,1)}) %all-reduce.5.cloned.1.call-update) | async-done | bytes 2359312 | tf_op jit(solution)/shard_map/psum | solution.py:84
  580.9 4.4 convert_multiply_fusion
  585.4 0.0 copy-done.1
  (2 shorter events, 0.0 us)
Async XLA Ops:
  7.2 388.6 %copy-start = (bf16[256,256]{1,0:T(8,128)(2,1)S(1)}, bf16[256,256]{1,0:T(8,128)(2,1)}, u32[]{:S(2)}) copy-start(bf16[256,256]{1,0:T(8,128)(2,1)} %param.16) | copy-start | bytes 393220
  9.7 35.8 %all-to-all-start.1 = ((bf16[24,128,128]{2,0,1:T(8,128)(2,1)}), bf16[24,128,128]{2,0,1:T(8,128)(2,1)S(1)}, u32[]{:S(2)}, u32[]{:S(2)}) async-start(bf16[24,128,128]{2,0,1:T(8,128)(2,1)} %copy.27), calls=%async_computation.1 | async-start | bytes 1572864 | tf_op jit(solution)/shard_map/all_to_all | solution.py:43
  45.6 6.5 %copy-start.4 = (f32[128]{0:T(128)S(1)}, f32[128]{0:T(128)}, u32[]{:S(2)}) copy-start(f32[128]{0:T(128)} %param.12) | copy-start | bytes 1540
  45.6 143.8 %all-to-all-start = ((bf16[4,24,2,128,128]{4,2,1,0,3:T(2,128)(2,1)}), bf16[4,24,2,128,128]{4,2,1,0,3:T(2,128)(2,1)}, u32[]{:S(2)}, u32[]{:S(2)}) async-start(bf16[4,24,2,128,128]{4,2,1,0,3:T(2,128)(2,1)} %copy.24), calls=%async_computation | async-start | bytes 12582912 | tf_op jit(solution)/shard_map/all_to_all | solution.py:51
  51.7 459.1 %all-reduce.3.cloned.1.call-start = ((), (), s32[]{:S(2)}) async-start(), calls=%async_computation.3 | async-start | bytes 4718592 | tf_op jit(solution)/shard_map/psum | solution.py:80
  368.0 6.5 %copy-start.2 = (f32[384,4,24,128]{3,0,2,1:T(8,128)}, f32[384,4,24,128]{3,0,2,1:T(8,128)S(1)}, u32[]{:S(2)}) copy-start(f32[384,4,24,128]{3,0,2,1:T(8,128)S(1)} %fusion.25) | copy-start | bytes 56623108
  374.5 4.3 copy-start.3
  378.8 17.0 %copy-start.5 = (bf16[128,256]{1,0:T(8,128)(2,1)S(1)}, bf16[128,256]{1,0:T(8,128)(2,1)}, u32[]{:S(2)}) copy-start(bf16[128,256]{1,0:T(8,128)(2,1)} %param.14) | copy-start | bytes 196612
  378.8 17.0 %copy-start.7 = (f32[256]{0:T(256)S(1)}, f32[256]{0:T(256)}, u32[]{:S(2)}) copy-start(f32[256]{0:T(256)} %param.15) | copy-start | bytes 3076
  395.8 27.9 %copy-start.6 = (bf16[256,128]{1,0:T(8,128)(2,1)S(1)}, bf16[256,128]{1,0:T(8,128)(2,1)}, u32[]{:S(2)}) copy-start(bf16[256,128]{1,0:T(8,128)(2,1)} %param.17) | copy-start | bytes 196612
  455.9 125.0 %all-reduce.5.cloned.1.call-start = ((), (), s32[]{:S(2)}) async-start(), calls=%async_computation.4 | async-start | bytes 4718592 | tf_op jit(solution)/shard_map/psum | solution.py:84
  510.8 74.6 %copy-start.1 = (bf16[256,256]{1,0:T(8,128)(2,1)S(1)}, bf16[256,256]{1,0:T(8,128)(2,1)}, u32[]{:S(2)}) copy-start(bf16[256,256]{1,0:T(8,128)(2,1)} %param.16) | copy-start | bytes 393220
Sparse Core Ops, SparseCore 0:
  456.1 54.6 all-reduce.2
  525.2 55.7 all-reduce.4
where the time goes:
time: 597 us; the launch traced here: 593 us
  waiting for transfers between devices  248 us (42%)
  blocking collectives  142 us (24%)
  matrix products  88.1 us (15%)
  local copies, waits for them, and re-layouts  55.2 us (9%)
  other arithmetic  31.5 us (5%)
  between operations  14.6 us (2%)
  starting transfers between devices  13.7 us (2%)
    all_to_all x1, blocking collectives, per_device(): lax.all_to_all(banded_grid, 'lat', split_axis=1, concat_axis=3, tiled=True)  142 us
    all_to_all x1, waiting for transfers between devices, per_device(): lax.all_to_all(fourier, 'lat', split_axis=3, concat_axis=1, tiled=True)  137 us
    psum x1, waiting for transfers between devices, per_device(): lax.psum(jnp.sum(jnp.square(member_values - ens_mean), axis=0).astype(jnp...  55.9 us
    psum x1, waiting for transfers between devices, per_device(): lax.psum(jnp.sum(member_values, axis=0).astype(jnp.bfloat16), 'grp')  54.8 us
    dot_general x1, matrix products, per_device(): jnp.dot(hidden_one, middle_weight, preferred_element_type=jnp.float32)  27.9 us
    dot_general x1, matrix products, per_device(): jnp.dot(hidden_two, output_weight, preferred_element_type=jnp.float32)  24.7 us
    reshape x1, local copies, waits for them, and re-layouts, per_device(): fourier = fourier.reshape(members, lat_rows, 2, wave_count, channels)  20.3 us
    dot_general x1, matrix products, per_device(): jnp.dot(smoothed_in, input_weight, preferred_element_type=jnp.float32)  16.9 us
  transfers between devices with their start and end apart: 4, of which 3 were waited for; matrix products, arithmetic and copies ran while one was open for 5% of the time, Pallas kernels for 0%

commit v1 on v0

v1 whole, which is shorter than its diff:
```python
import functools
import math

import jax
import jax.numpy as jnp
from jax import lax
from jax.experimental import pallas as pl
from jax.experimental.pallas import tpu as pltpu
from jax.sharding import PartitionSpec as P

BF16 = jnp.bfloat16
F32 = jnp.float32


def wave_table(lon_count, wave_count):
    lon_ids = jnp.arange(lon_count, dtype=jnp.int32)[:, None]
    wave_ids = jnp.arange(wave_count, dtype=jnp.int32)[None, :]
    phase = (lon_ids * wave_ids % lon_count).astype(jnp.float32) * (2.0 * math.pi / lon_count)
    factor = math.sqrt(2.0 / lon_count)
    joined = jnp.concatenate([jnp.cos(phase), -jnp.sin(phase)], axis=1) * factor
    return joined.astype(jnp.bfloat16)


def damping_filter(diffusion, wave_count):
    degree = jnp.arange(wave_count, dtype=jnp.int32).astype(jnp.float32)
    ratio = degree * (degree + 1.0) / float((wave_count - 1) * wave_count)
    return 1.0 / (1.0 + diffusion[None, :] * (ratio * ratio)[:, None])


def analysis_body(table_ref, grid_ref, out_ref):
    bands, _, rows, width, channels = out_ref.shape
    for row in range(0, rows, 2):
        pair = jnp.concatenate([grid_ref[0, row], grid_ref[0, row + 1]], axis=1)
        waves = jnp.dot(table_ref[...], pair, preferred_element_type=F32).astype(BF16)
        for k in range(2):
            out_ref[:, 0, row + k] = waves[:, k * channels:(k + 1) * channels].reshape(
                bands, width, channels
            )


def analyse(grid_state, table, first, count, bands):
    _, lat_rows, lon_count, channels = grid_state.shape
    width = table.shape[0] // bands
    rows = 6
    return pl.pallas_call(
        analysis_body,
        grid=(count, lat_rows // rows),
        in_specs=[
            pl.BlockSpec(table.shape, lambda b, i: (0, 0)),
            pl.BlockSpec((1, rows, lon_count, channels), lambda b, i: (b + first, i, 0, 0)),
        ],
        out_specs=pl.BlockSpec((bands, 1, rows, width, channels), lambda b, i: (0, b, i, 0, 0)),
        out_shape=jax.ShapeDtypeStruct((bands, count, lat_rows, width, channels), BF16),
        cost_estimate=pl.CostEstimate(
            flops=2 * count * lat_rows * lon_count * channels * table.shape[0],
            bytes_accessed=4 * count * lat_rows * lon_count * channels,
            transcendentals=0,
        ),
    )(table, grid_state)


def spectral_body(parts, in_ref, basis_ref, flipped_ref, damping_ref, *rest):
    outs, (fin, fout) = rest[:parts], rest[parts:]
    bands, _, lat_rows, width, channels = in_ref.shape
    waves = basis_ref.shape[0]
    lats = bands * lat_rows
    span = lat_rows * width
    for s in range(bands):
        fin[pl.ds(s * span, span), :] = in_ref[s, 0].astype(F32).reshape(span, channels)
    damping = jnp.concatenate([damping_ref[...]] * 2, axis=1)
    for m in range(waves):
        values = jnp.concatenate(
            [fin[pl.ds(r * waves + m, lats, stride=width), :] for r in range(2)], axis=1
        ).astype(BF16)
        spectrum = jnp.dot(flipped_ref[m], values, preferred_element_type=F32)
        filtered = (spectrum * damping).astype(BF16)
        grid = jnp.dot(basis_ref[m], filtered, preferred_element_type=F32)
        for r in range(2):
            fout[pl.ds(r * waves + m, lats, stride=width), :] = grid[
                :, r * channels:(r + 1) * channels
            ]
    part_rows = lat_rows // parts
    for q in range(parts):
        for s in range(bands):
            start = (s * lat_rows + q * part_rows) * width
            outs[q][s, 0] = (
                fout[pl.ds(start, part_rows * width), :]
                .reshape(part_rows, width, channels)
                .astype(BF16)
            )


def spectral(received, basis, flipped, damping, parts):
    bands, count, lat_rows, width, channels = received.shape
    part_rows = lat_rows // parts
    whole = lambda a: pl.BlockSpec(a.shape, lambda b: (0,) * a.ndim)
    return pl.pallas_call(
        functools.partial(spectral_body, parts),
        grid=(count,),
        in_specs=[
            pl.BlockSpec((bands, 1, lat_rows, width, channels), lambda b: (0, b, 0, 0, 0)),
            whole(basis),
            whole(flipped),
            whole(damping),
        ],
        out_specs=[
            pl.BlockSpec((bands, 1, part_rows, width, channels), lambda b: (0, b, 0, 0, 0))
        ] * parts,
        out_shape=[
            jax.ShapeDtypeStruct((bands, count, part_rows, width, channels), BF16)
        ] * parts,
        scratch_shapes=[pltpu.VMEM((bands * lat_rows * width, channels), F32)] * 2,
        cost_estimate=pl.CostEstimate(
            flops=8 * count * basis.size * channels,
            bytes_accessed=4 * received.size,
            transcendentals=0,
        ),
    )(received, basis, flipped, damping)


def silu(value):
    half = 0.5 * value
    return half + half * jnp.tanh(half)


def physics_body(groups, *refs):
    fields = refs[:groups]
    noise_ref, table_ref, first_ref, bias_ref, middle_ref, last_ref = refs[groups:groups + 6]
    state_ref, stats_ref = refs[-2:]
    members, _, lon_count, channels = noise_ref.shape
    states = []
    for ref in fields:
        count = ref.shape[1]
        waves = jnp.concatenate(
            [ref[:, k, 0].reshape(-1, channels) for k in range(count)], axis=1
        )
        smoothed = jnp.dot(table_ref[...], waves, preferred_element_type=F32)
        for k in range(count):
            flat = smoothed[:, k * channels:(k + 1) * channels]
            b = len(states)
            joined = jnp.concatenate([flat.astype(BF16), noise_ref[b, 0]], axis=1)
            pre = jnp.dot(joined, first_ref[...], preferred_element_type=F32)
            one = silu(pre + bias_ref[...]).astype(BF16)
            two = silu(jnp.dot(one, middle_ref[...], preferred_element_type=F32)).astype(BF16)
            tendency = jnp.dot(two, last_ref[...], preferred_element_type=F32)
            state = (flat + tendency).astype(BF16)
            state_ref[b, 0] = state
            states.append(state)
    values = [s.astype(F32) for s in states]
    total = functools.reduce(jnp.add, values)
    mean = total * (1.0 / members)
    spread = functools.reduce(jnp.add, [jnp.square(v - mean) for v in values])
    half = lon_count // 2
    for h in range(2):
        stats_ref[h, 0, 0] = total[h * half:(h + 1) * half].astype(BF16)
        stats_ref[h, 1, 0] = spread[h * half:(h + 1) * half].astype(BF16)


def physics(fields, noise, table, first, bias, middle, last, part, previous):
    bands, _, part_rows, width, channels = fields[0].shape
    members, lat_rows, lon_count, noise_channels = noise.shape
    whole = lambda a: pl.BlockSpec(a.shape, lambda i: (0,) * a.ndim)
    at = part * part_rows
    specs = [
        pl.BlockSpec((bands, f.shape[1], 1, width, channels), lambda i: (0, 0, i, 0, 0))
        for f in fields
    ]
    specs.append(
        pl.BlockSpec((members, 1, lon_count, noise_channels), lambda i: (0, i + at, 0, 0))
    )
    params = [table, first, bias, middle, last]
    specs += [whole(a) for a in params]
    operands = [*fields, noise, *params]
    aliases = {}
    if previous is not None:
        aliases = {len(operands): 0}
        operands.append(previous)
        specs.append(pl.BlockSpec(memory_space=pl.ANY))
    columns = members * part_rows * lon_count
    hidden = middle.shape[0]
    return pl.pallas_call(
        functools.partial(physics_body, len(fields)),
        grid=(part_rows,),
        in_specs=specs,
        out_specs=[
            pl.BlockSpec((members, 1, lon_count, channels), lambda i: (0, i + at, 0, 0)),
            pl.BlockSpec((2, 2, 1, lon_count // 2, channels), lambda i: (0, 0, i, 0, 0)),
        ],
        out_shape=[
            jax.ShapeDtypeStruct((members, lat_rows, lon_count, channels), BF16),
            jax.ShapeDtypeStruct((2, 2, part_rows, lon_count // 2, channels), BF16),
        ],
        input_output_aliases=aliases,
        cost_estimate=pl.CostEstimate(
            flops=2 * columns * (first.size + middle.size + last.size + 256 * channels),
            bytes_accessed=8 * columns * channels,
            transcendentals=2 * columns * hidden,
        ),
    )(*operands)


def ensemble_moments(stats, members):
    groups = lax.axis_size("grp")
    core = lax.axis_index("grp") % 2

    def swap(value, bit):
        return lax.ppermute(value, "grp", [(g, g ^ bit) for g in range(groups)])

    def join(a, b, count):
        a, b = a.astype(F32), b.astype(F32)
        total = a[0] + b[0]
        spread = (a[1] + b[1]) + jnp.square(a[0] - b[0]) * (0.5 / count)
        return jnp.stack([total, spread])

    own = lax.dynamic_index_in_dim(stats, core, 0, keepdims=False)
    other = lax.dynamic_index_in_dim(stats, 1 - core, 0, keepdims=False)
    held = join(own, swap(other, 1), members)
    bit, count = 2, 2 * members
    while bit < groups:
        held = held.astype(BF16)
        held = join(held, swap(held, bit), count)
        bit, count = 2 * bit, 2 * count
    scale = jnp.array([1.0 / count, 1.0 / (count - 1)], F32)
    held = (held * scale[:, None, None, None]).astype(BF16)
    partner = swap(held, 1)
    low = jnp.where(core == 0, held, partner)
    high = jnp.where(core == 0, partner, held)
    return low, high


def per_device(
    grid_state,
    noise_field,
    legendre,
    diffusion,
    input_weight,
    noise_weight,
    input_bias,
    middle_weight,
    output_weight,
):
    members, lat_rows, lon_count, channels = grid_state.shape
    wave_count = legendre.shape[1]
    bands = lax.axis_size("lat")
    local_waves = wave_count // bands
    chunk = 2
    parts = 2
    transform = wave_table(lon_count, wave_count)
    table = (
        transform.reshape(lon_count, 2, bands, local_waves)
        .transpose(0, 2, 1, 3)
        .reshape(lon_count, 2 * wave_count)
    )
    table_t = table.T
    exchange = lambda v: lax.all_to_all(v, "lat", split_axis=0, concat_axis=0, tiled=True)
    damping = damping_filter(diffusion, wave_count)

    sent = [
        analyse(grid_state, table_t, b, chunk, bands) for b in range(0, members, chunk)
    ]
    basis = lax.all_to_all(legendre, "lat", split_axis=1, concat_axis=0, tiled=True)
    zonal_ids = lax.axis_index("lat") * local_waves + jnp.arange(local_waves, dtype=jnp.int32)
    total_ids = jnp.arange(wave_count, dtype=jnp.int32)
    triangle = total_ids[None, :] >= zonal_ids[:, None]
    basis = jnp.where(triangle[None], basis, jnp.zeros_like(basis)).transpose(1, 0, 2)
    flipped = basis.transpose(0, 2, 1)
    received = [exchange(s) for s in sent]
    banded = [spectral(r, basis, flipped, damping, parts) for r in received]

    first = jnp.concatenate([input_weight, noise_weight], axis=0)
    new_state = None
    moments = []
    for q in range(parts):
        fields = [exchange(g[q]) for g in banded]
        new_state, stats = physics(
            fields, noise_field, table, first, input_bias[None], middle_weight,
            output_weight, q, new_state,
        )
        moments.append(ensemble_moments(stats, members))
    joined = [jnp.concatenate([low, high], axis=2) for low, high in moments]
    ens_mean = jnp.concatenate([j[0] for j in joined], axis=0).astype(F32)
    ens_var = jnp.concatenate([j[1] for j in joined], axis=0).astype(F32)
    return (new_state, ens_mean, ens_var)


def solution(mesh):
    in_specs = (
        P("grp", "lat", None, None),
        P("grp", "lat", None, None),
        P("lat", None, None),
        P(),
        P(),
        P(),
        P(),
        P(),
        P(),
    )
    out_specs = (P("grp", "lat", None, None), P("lat", None, None), P("lat", None, None))
    return jax.shard_map(
        per_device, mesh=mesh, in_specs=in_specs, out_specs=out_specs, check_vma=False
    )
```

time: 597 us -> 434 us (0.73)
  matrix products: 88.1 us -> 0 us
  Pallas kernels: 0 us -> 80.3 us
  blocking collectives: 142 us -> 81.9 us
  local copies, waits for them, and re-layouts: 55.2 us -> 13.5 us
  waiting for transfers between devices: 248 us -> 210 us
  between operations: 14.6 us -> 0.92 us
  starting transfers between devices: 13.7 us -> 26.6 us
  other arithmetic: 31.5 us -> 19.9 us
    psum x2 -> x0, waiting for transfers between devices: 111 us -> none  [the longest x1 55.9 us: per_device(): lax.psum(jnp.sum(jnp.square(member_values - ens_mean), axis=0).astype(jnp...]
    dot_general x6 -> x0, matrix products: 88.1 us -> none  [the longest x1 27.9 us: per_device(): jnp.dot(hidden_one, middle_weight, preferred_element_type=jnp.float32)]
    pallas_call x0 -> x6, Pallas kernels: none -> 80.3 us  [the longest x2 41.2 us: physics(): pl.pallas_call(functools.partial(physics_body, len(fields)), grid=(part_r...]
    all_to_all x1 -> x2, blocking collectives: 142 us -> 81.9 us  [per_device(): lax.all_to_all(v, 'lat', split_axis=0, concat_axis=0, tiled=True)]
    ppermute x0 -> x6, waiting for transfers between devices: none -> 51.5 us  [swap(): return lax.ppermute(value, 'grp', [(g, g ^ bit) for g in range(groups)])]
    reshape x1, local copies, waits for them, and re-layouts: 20.3 us -> 0.84 us  [per_device(): table = transform.reshape(lon_count, 2, bands, local_waves).transpose(0,...]
    reduce_sum x2 -> x0, other arithmetic: 17.3 us -> none  [the longest x1 9.77 us: per_device(): jnp.sum(jnp.square(member_values - ens_mean), axis=0).astype(jnp.bfloat16)]
    all_to_all x3 -> x0, local copies, waits for them, and re-layouts: 16.3 us -> none  [the longest x2 14.4 us: per_device(): lax.all_to_all(fourier, 'lat', split_axis=3, concat_axis=1, tiled=True)]
  transfers between devices with their start and end apart: 4 -> 11, of which waited for: 3 -> 9; matrix products, arithmetic and copies ran while one was open for 5% -> 5% of each run, Pallas kernels for 0% -> 19%
where the time goes in v1:
time: 434 us; the launch traced here: 433 us
  waiting for transfers between devices  210 us (48%)
  blocking collectives  81.9 us (19%)
  Pallas kernels  80.3 us (19%)
  starting transfers between devices  26.6 us (6%)
  other arithmetic  19.9 us (5%)
  local copies, waits for them, and re-layouts  13.5 us (3%)
    all_to_all x4, waiting for transfers between devices, per_device(): lax.all_to_all(v, 'lat', split_axis=0, concat_axis=0, tiled=True)  148 us
    all_to_all x2, blocking collectives, per_device(): lax.all_to_all(v, 'lat', split_axis=0, concat_axis=0, tiled=True)  81.9 us
    ppermute x6, waiting for transfers between devices, swap(): return lax.ppermute(value, 'grp', [(g, g ^ bit) for g in range(groups)])  51.5 us
    pallas_call x2, Pallas kernels, physics(): pl.pallas_call(functools.partial(physics_body, len(fields)), grid=(part_r...  41.2 us
    pallas_call x2, Pallas kernels, spectral(): pl.pallas_call(functools.partial(spectral_body, parts), grid=(count,), in...  23.7 us
    all_to_all x4, starting transfers between devices, per_device(): lax.all_to_all(v, 'lat', split_axis=0, concat_axis=0, tiled=True)  15.5 us
    pallas_call x2, Pallas kernels, analyse(): pl.pallas_call(analysis_body, grid=(count, lat_rows // rows), in_specs=[p...  15.4 us
    all_to_all x1, waiting for transfers between devices, per_device(): lax.all_to_all(legendre, 'lat', split_axis=1, concat_axis=0, tiled=True)  10.8 us
  transfers between devices with their start and end apart: 11, of which 9 were waited for; matrix products, arithmetic and copies ran while one was open for 5% of the time, Pallas kernels for 19%

profile of v1, /device:TPU:0, one launch (start us, length us, event | category | flops | bytes accessed | tf_op | source)
XLA Modules:
  0.0 433.2 jit_solution(14392588963136440355)
XLA Ops:
  0.6 2.5 copy.31
  3.2 7.3 %all-to-all-start.1 = ((bf16[24,128,128]{2,0,1:T(8,128)(2,1)}), bf16[24,128,128]{2,0,1:T(8,128)(2,1)S(1)}, u32[]{:S(2)}, u32[]{:S(2)}) async-start(bf16[24,128,128]{2,0,1:T(8,128)(2,1)} %copy.31), calls=%async_computation.1 | async-start | bytes 1572864 | tf_op jit(solution)/shard_map/all_to_all | solution.py:261
  10.5 0.9 fusion.21
  11.4 0.7 fusion.16
  12.1 7.7 %shard_map.130 = bf16[8,2,24,32,128]{4,3,2,1,0:T(8,128)(2,1)} custom-call(bf16[256,384]{1,0:T(8,128)(2,1)} %bitcast.48, bf16[4,24,384,128]{3,2,1,0:T(8,128)(2,1)} %grid_ref.3), custom_call_target="tpu_custom_call" | custom-call | flops 1207959552 | bytes 9437184 | tf_op jit(solution)/shard_map/pallas_call | solution.py:45
  19.8 10.8 %all-to-all-done.1 = bf16[24,128,128]{2,0,1:T(8,128)(2,1)S(1)} async-done(((bf16[24,128,128]{2,0,1:T(8,128)(2,1)}), bf16[24,128,128]{2,0,1:T(8,128)(2,1)S(1)}, u32[]{:S(2)}, u32[]{:S(2)}) %all-to-all-start.1) | async-done | bytes 786464 | tf_op jit(solution)/shard_map/all_to_all | solution.py:261
  30.6 0.9 copy-done.2
  31.5 3.7 all-to-all-start
  35.2 7.7 %shard_map.132 = bf16[8,2,24,32,128]{4,3,2,1,0:T(8,128)(2,1)} custom-call(bf16[256,384]{1,0:T(8,128)(2,1)} %bitcast.49, bf16[4,24,384,128]{3,2,1,0:T(8,128)(2,1)} %grid_ref.3), custom_call_target="tpu_custom_call" | custom-call | flops 1207959552 | bytes 9437184 | tf_op jit(solution)/shard_map/pallas_call | solution.py:45
  42.9 63.1 %all-to-all-done.in_ref = bf16[8,2,24,32,128]{4,3,2,1,0:T(8,128)(2,1)S(1)} async-done(((bf16[8,2,24,32,128]{4,3,2,1,0:T(8,128)(2,1)}), bf16[8,2,24,32,128]{4,3,2,1,0:T(8,128)(2,1)S(1)}, u32[]{:S(2)}, u32[]{:S(2)}) %all-to-all-start) | async-done | bytes 3145760 | tf_op jit(solution)/shard_map/all_to_all | solution.py:255
  106.0 1.7 copy-done.1
  107.7 3.7 all-to-all-start.3
  111.3 0.1 iota_compare_fusion
  111.4 0.7 add_divide_fusion.damping_ref
  112.1 2.2 copy.33
  114.3 2.3 copy.34
  116.6 2.6 fusion.14
  119.2 2.2 copy.35.basis_ref
  121.4 11.8 %shard_map.131 = (bf16[8,2,12,32,128]{4,3,2,1,0:T(8,128)(2,1)}, bf16[8,2,12,32,128]{4,3,2,1,0:T(8,128)(2,1)}) custom-call(bf16[8,2,24,32,128]{4,3,2,1,0:T(8,128)(2,1)} %copy-done.1, bf16[16,192,128]{2,1,0:T(8,128)(2,1)} %copy.35.basis_ref, bf16[16,128,192]{2,1,0:T(8,128)(2,1)} %get-tuple-element.43.flipped_ref, f32[128,128]{1,0:T(8,128)} %add_divide_fusion.damping_ref), custom_call_target="tpu_custom_call" | custom-call | flops 805306368 | bytes 6291456 | tf_op jit(solution)/shard_map/pallas_call | solution.py:97
  133.2 49.0 %all-to-all-done.3.in_ref = bf16[8,2,24,32,128]{4,3,2,1,0:T(8,128)(2,1)S(1)} async-done(((bf16[8,2,24,32,128]{4,3,2,1,0:T(8,128)(2,1)}), bf16[8,2,24,32,128]{4,3,2,1,0:T(8,128)(2,1)S(1)}, u32[]{:S(2)}, u32[]{:S(2)}) %all-to-all-start.3) | async-done | bytes 3145760 | tf_op jit(solution)/shard_map/all_to_all | solution.py:255
  182.2 41.0 %all_to_all.48.refs_0_ = bf16[8,2,12,32,128]{4,3,2,1,0:T(8,128)(2,1)} all-to-all(bf16[8,2,12,32,128]{4,3,2,1,0:T(8,128)(2,1)} %get-tuple-element.11), channel_id=1, replica_groups=mesh['grp'=4,'lat'=8] {'lat'}, dimensions={0} | all-to-all | bytes 3145728 | tf_op jit(solution)/shard_map/all_to_all | solution.py:255
  223.1 3.8 all-to-all-start.5
  226.9 11.9 %shard_map.133 = (bf16[8,2,12,32,128]{4,3,2,1,0:T(8,128)(2,1)}, bf16[8,2,12,32,128]{4,3,2,1,0:T(8,128)(2,1)}) custom-call(bf16[8,2,24,32,128]{4,3,2,1,0:T(8,128)(2,1)} %copy-done, bf16[16,192,128]{2,1,0:T(8,128)(2,1)} %copy.35.basis_ref, bf16[16,128,192]{2,1,0:T(8,128)(2,1)} %get-tuple-element.43.flipped_ref, f32[128,128]{1,0:T(8,128)} %add_divide_fusion.damping_ref), custom_call_target="tpu_custom_call" | custom-call | flops 805306368 | bytes 6291456 | tf_op jit(solution)/shard_map/pallas_call | solution.py:97
  238.8 24.6 %all-to-all-done.5.refs_0_ = bf16[8,2,12,32,128]{4,3,2,1,0:T(8,128)(2,1)S(1)} async-done(((bf16[8,2,12,32,128]{4,3,2,1,0:T(8,128)(2,1)}), bf16[8,2,12,32,128]{4,3,2,1,0:T(8,128)(2,1)S(1)}, u32[]{:S(2)}, u32[]{:S(2)}) %all-to-all-start.5) | async-done | bytes 1572896 | tf_op jit(solution)/shard_map/all_to_all | solution.py:255
  263.4 40.9 %all_to_all.49.refs_1_ = bf16[8,2,12,32,128]{4,3,2,1,0:T(8,128)(2,1)} all-to-all(bf16[8,2,12,32,128]{4,3,2,1,0:T(8,128)(2,1)} %get-tuple-element.14), channel_id=1, replica_groups=mesh['grp'=4,'lat'=8] {'lat'}, dimensions={0} | all-to-all | bytes 3145728 | tf_op jit(solution)/shard_map/all_to_all | solution.py:255
  304.2 0.0 copy-done.4
  304.3 4.4 %all-to-all-start.4 = ((bf16[8,2,12,32,128]{4,3,2,1,0:T(8,128)(2,1)}), bf16[8,2,12,32,128]{4,3,2,1,0:T(8,128)(2,1)}, u32[]{:S(2)}, u32[]{:S(2)}) async-start(bf16[8,2,12,32,128]{4,3,2,1,0:T(8,128)(2,1)} %get-tuple-element.12), calls=%async_computation.4 | async-start | bytes 3145728 | tf_op jit(solution)/shard_map/all_to_all | solution.py:255
  308.7 0.8 copy.38.refs_3_
  309.6 0.6 copy-done.7
  310.3 20.4 %shard_map.134 = (bf16[4,24,384,128]{3,2,1,0:T(8,128)(2,1)}, bf16[2,2,12,192,128]{4,3,2,1,0:T(8,128)(2,1)}) custom-call(bf16[8,2,12,32,128]{4,3,2,1,0:T(8,128)(2,1)} %copy-done.4, bf16[8,2,12,32,128]{4,3,2,1,0:T(8,128)(2,1)} %all_to_all.49.refs_1_, bf16[4,24,384,128]{3,2,1,0:T(8,128)(2,1)} %refs_2_.3, bf16[384,256]{1,0:T(8,128)(2,1)} %copy.38.refs_3_, ...), custom_call_target="tpu_custom_call" | custom-call | flops 7247757312 | bytes 18874368 | tf_op jit(solution)/shard_map/pallas_call | solution.py:181
  330.7 2.9 dynamic-slice_convert_fusion.1
  333.6 0.0 collective-permute-start
  333.6 11.2 %all-to-all-done.4.refs_1_ = bf16[8,2,12,32,128]{4,3,2,1,0:T(8,128)(2,1)} async-done(((bf16[8,2,12,32,128]{4,3,2,1,0:T(8,128)(2,1)}), bf16[8,2,12,32,128]{4,3,2,1,0:T(8,128)(2,1)}, u32[]{:S(2)}, u32[]{:S(2)}) %all-to-all-start.4) | async-done | bytes 1572896 | tf_op jit(solution)/shard_map/all_to_all | solution.py:255
  344.8 20.7 %shard_map.135 = (bf16[4,24,384,128]{3,2,1,0:T(8,128)(2,1)}, bf16[2,2,12,192,128]{4,3,2,1,0:T(8,128)(2,1)}) custom-call(bf16[8,2,12,32,128]{4,3,2,1,0:T(8,128)(2,1)} %all_to_all.48.refs_0_, bf16[8,2,12,32,128]{4,3,2,1,0:T(8,128)(2,1)} %all-to-all-done.4.refs_1_, bf16[4,24,384,128]{3,2,1,0:T(8,128)(2,1)} %refs_2_.3, ...), custom_call_target="tpu_custom_call", output_to_operand_aliasing={{0}: (8, {})} | custom-call | flops 7247757312 | bytes 18874368 | tf_op jit(solution)/shard_map/pallas_call | solution.py:181
  365.6 1.9 dynamic-slice_convert_fusion
  367.5 0.1 collective-permute-start.3
  367.6 0.0 collective-permute-done
  367.6 0.2 convert_element_type.68
  367.8 0.5 add_convert_fusion.1
  368.3 0.2 fusion.26
  368.5 1.6 collective-permute-start.1
  370.1 0.3 collective-permute-done.3
  370.4 0.2 convert_element_type.73
  370.7 0.4 add_convert_fusion
  371.1 0.2 fusion.25
  371.3 1.6 collective-permute-start.4
  372.9 24.6 %collective-permute-done.1 = bf16[2,12,192,128]{3,2,1,0:T(8,128)(2,1)S(1)} collective-permute-done((bf16[2,12,192,128]{3,2,1,0:T(8,128)(2,1)S(1)}, bf16[2,12,192,128]{3,2,1,0:T(8,128)(2,1)S(1)}, u32[]{:S(2)}, u32[]{:S(2)}) %collective-permute-start.1) | collective-permute-done | bytes 1179680 | tf_op jit(solution)/shard_map/ppermute | solution.py:207
  397.4 0.2 convert_element_type.70
  397.7 0.4 slice_add_fusion.5
  398.1 24.1 %collective-permute-done.4 = bf16[2,12,192,128]{3,2,1,0:T(8,128)(2,1)S(1)} collective-permute-done((bf16[2,12,192,128]{3,2,1,0:T(8,128)(2,1)S(1)}, bf16[2,12,192,128]{3,2,1,0:T(8,128)(2,1)S(1)}, u32[]{:S(2)}, u32[]{:S(2)}) %collective-permute-start.4) | collective-permute-done | bytes 1179680 | tf_op jit(solution)/shard_map/ppermute | solution.py:207
  422.2 0.2 convert_element_type.75
  422.5 0.0 copy-start.9
  422.5 0.4 slice_add_fusion.4
  423.0 0.2 copy-done.9
  423.2 0.6 fusion
  423.8 0.1 collective-permute-start.5
  423.9 0.5 collective-permute-start.2
  424.4 2.5 collective-permute-done.5
  426.9 1.4 broadcast_select_fusion
  428.3 0.2 fusion.6
  428.5 0.0 collective-permute-done.2
  428.5 0.2 broadcast_select_fusion.2
  428.6 0.2 fusion.7
  428.8 4.3 %maximum_convert_fusion = (f32[24,384,128]{2,1,0:T(8,128)}, f32[24,384,128]{2,1,0:T(8,128)}) fusion(bf16[12,384,128]{2,1,0:T(8,128)(2,1)S(1)} %get-tuple-element.30, bf16[12,384,128]{2,1,0:T(8,128)(2,1)S(1)} %get-tuple-element.28, bf16[12,384,128]{2,1,0:T(8,128)(2,1)S(1)} %get-tuple-element.29, bf16[12,384,128]{2,1,0:T(8,128)(2,1)S(1)} %get-tuple-element.27), kind=kLoop, calls=%fused_computation.8 | loop fusion | flops 4718592 | bytes 14155776 | tf_op jit(solution)/shard_map/convert_element_type | solution.py:281
  (19 shorter events, 0.1 us)
Async XLA Ops:
  3.2 27.5 %all-to-all-start.1 = ((bf16[24,128,128]{2,0,1:T(8,128)(2,1)}), bf16[24,128,128]{2,0,1:T(8,128)(2,1)S(1)}, u32[]{:S(2)}, u32[]{:S(2)}) async-start(bf16[24,128,128]{2,0,1:T(8,128)(2,1)} %copy.31), calls=%async_computation.1 | async-start | bytes 1572864 | tf_op jit(solution)/shard_map/all_to_all | solution.py:261
  30.6 0.9 copy-start.2
  31.5 74.5 %all-to-all-start = ((bf16[8,2,24,32,128]{4,3,2,1,0:T(8,128)(2,1)}), bf16[8,2,24,32,128]{4,3,2,1,0:T(8,128)(2,1)S(1)}, u32[]{:S(2)}, u32[]{:S(2)}) async-start(bf16[8,2,24,32,128]{4,3,2,1,0:T(8,128)(2,1)} %shard_map.130), calls=%async_computation | async-start | bytes 6291456 | tf_op jit(solution)/shard_map/all_to_all | solution.py:255
  42.9 68.5 %copy-start.8 = (f32[128]{0:T(128)S(1)}, f32[128]{0:T(128)}, u32[]{:S(2)}) copy-start(f32[128]{0:T(128)} %param.14) | copy-start | bytes 1540
  106.0 1.7 copy-start.1
  107.7 74.5 %all-to-all-start.3 = ((bf16[8,2,24,32,128]{4,3,2,1,0:T(8,128)(2,1)}), bf16[8,2,24,32,128]{4,3,2,1,0:T(8,128)(2,1)S(1)}, u32[]{:S(2)}, u32[]{:S(2)}) async-start(bf16[8,2,24,32,128]{4,3,2,1,0:T(8,128)(2,1)} %shard_map.132), calls=%async_computation.3 | async-start | bytes 6291456 | tf_op jit(solution)/shard_map/all_to_all | solution.py:255
  182.2 41.0 %copy-start = (bf16[8,2,24,32,128]{4,3,2,1,0:T(8,128)(2,1)}, bf16[8,2,24,32,128]{4,3,2,1,0:T(8,128)(2,1)S(1)}, u32[]{:S(2)}) copy-start(bf16[8,2,24,32,128]{4,3,2,1,0:T(8,128)(2,1)S(1)} %all-to-all-done.3.in_ref) | copy-start | bytes 9437188
  223.1 40.2 %all-to-all-start.5 = ((bf16[8,2,12,32,128]{4,3,2,1,0:T(8,128)(2,1)}), bf16[8,2,12,32,128]{4,3,2,1,0:T(8,128)(2,1)S(1)}, u32[]{:S(2)}, u32[]{:S(2)}) async-start(bf16[8,2,12,32,128]{4,3,2,1,0:T(8,128)(2,1)} %get-tuple-element.13), calls=%async_computation.5 | async-start | bytes 3145728 | tf_op jit(solution)/shard_map/all_to_all | solution.py:255
  263.4 40.9 %copy-start.4 = (bf16[8,2,12,32,128]{4,3,2,1,0:T(8,128)(2,1)}, bf16[8,2,12,32,128]{4,3,2,1,0:T(8,128)(2,1)S(1)}, u32[]{:S(2)}) copy-start(bf16[8,2,12,32,128]{4,3,2,1,0:T(8,128)(2,1)S(1)} %all-to-all-done.5.refs_0_) | copy-start | bytes 4718596
  304.2 4.5 %copy-start.3 = (bf16[384,2,8,16]{0,3,1,2:T(8,128)(2,1)S(1)}, bf16[384,2,8,16]{0,3,1,2:T(8,128)(2,1)}, u32[]{:S(2)}) copy-start(bf16[384,2,8,16]{0,3,1,2:T(8,128)(2,1)} %fusion.16) | copy-start | bytes 589828
  304.2 5.3 %copy-start.5 = (bf16[128,256]{1,0:T(8,128)(2,1)S(1)}, bf16[128,256]{1,0:T(8,128)(2,1)}, u32[]{:S(2)}) copy-start(bf16[128,256]{1,0:T(8,128)(2,1)} %param.15) | copy-start | bytes 196612
  304.2 5.3 %copy-start.6 = (bf16[128,256]{1,0:T(8,128)(2,1)S(1)}, bf16[128,256]{1,0:T(8,128)(2,1)}, u32[]{:S(2)}) copy-start(bf16[128,256]{1,0:T(8,128)(2,1)} %param.16) | copy-start | bytes 196612
  304.3 40.6 %all-to-all-start.4 = ((bf16[8,2,12,32,128]{4,3,2,1,0:T(8,128)(2,1)}), bf16[8,2,12,32,128]{4,3,2,1,0:T(8,128)(2,1)}, u32[]{:S(2)}, u32[]{:S(2)}) async-start(bf16[8,2,12,32,128]{4,3,2,1,0:T(8,128)(2,1)} %get-tuple-element.12), calls=%async_computation.4 | async-start | bytes 3145728 | tf_op jit(solution)/shard_map/all_to_all | solution.py:255
  309.6 0.6 copy-start.7
  333.6 33.9 %collective-permute-start = (bf16[2,12,192,128]{3,2,1,0:T(8,128)(2,1)}, bf16[2,12,192,128]{3,2,1,0:T(8,128)(2,1)S(1)}, u32[]{:S(2)}, u32[]{:S(2)}) collective-permute-start(bf16[2,12,192,128]{3,2,1,0:T(8,128)(2,1)} %get-tuple-element.34), channel_id=1, source_target_pairs={{0,8},{8,0},{16,24},{24,16},{1,9},{9,1},{17,25},{25,17},{2,10},{10... | collective-permute-start | bytes 3538952 | tf_op jit(solution)/shard_map/ppermute | solution.py:207
  367.5 2.9 collective-permute-start.3
  368.5 28.9 %collective-permute-start.1 = (bf16[2,12,192,128]{3,2,1,0:T(8,128)(2,1)S(1)}, bf16[2,12,192,128]{3,2,1,0:T(8,128)(2,1)S(1)}, u32[]{:S(2)}, u32[]{:S(2)}) collective-permute-start(bf16[2,12,192,128]{3,2,1,0:T(8,128)(2,1)S(1)} %get-tuple-element.40), channel_id=1, source_target_pairs={{0,16},{8,24},{16,0},{24,8},{1,17},{9,25},{17,1},{25,9},{2,18},{10... | collective-permute-start | bytes 3538952 | tf_op jit(solution)/shard_map/ppermute | solution.py:207
  371.3 50.9 %collective-permute-start.4 = (bf16[2,12,192,128]{3,2,1,0:T(8,128)(2,1)S(1)}, bf16[2,12,192,128]{3,2,1,0:T(8,128)(2,1)S(1)}, u32[]{:S(2)}, u32[]{:S(2)}) collective-permute-start(bf16[2,12,192,128]{3,2,1,0:T(8,128)(2,1)S(1)} %get-tuple-element.42), channel_id=1, source_target_pairs={{0,16},{8,24},{16,0},{24,8},{1,17},{9,25},{17,1},{25,9},{2,18},{10... | collective-permute-start | bytes 3538952 | tf_op jit(solution)/shard_map/ppermute | solution.py:207
  422.5 0.7 copy-start.9
  423.8 3.0 collective-permute-start.5
  423.9 4.6 %collective-permute-start.2 = (bf16[2,12,192,128]{3,2,1,0:T(8,128)(2,1)S(1)}, bf16[2,12,192,128]{3,2,1,0:T(8,128)(2,1)S(1)}, u32[]{:S(2)}, u32[]{:S(2)}) collective-permute-start(bf16[2,12,192,128]{3,2,1,0:T(8,128)(2,1)S(1)} %get-tuple-element.47), channel_id=1, source_target_pairs={{0,8},{8,0},{16,24},{24,16},{1,9},{9,1},{17,25},{25,17},{2,10},{10... | collective-permute-start | bytes 3538952 | tf_op jit(solution)/shard_map/ppermute | solution.py:207

commit v2 on v1

--- a/solution.py
+++ b/solution.py
@@ -199,26 +199,31 @@
     )(*operands)
 
 
-def ensemble_moments(stats, members):
+def swap(value, bit):
+    groups = lax.axis_size("grp")
+    return lax.ppermute(value, "grp", [(g, g ^ bit) for g in range(groups)])
+
+
+def join(a, b, count):
+    a, b = a.astype(F32), b.astype(F32)
+    total = a[0] + b[0]
+    spread = (a[1] + b[1]) + jnp.square(a[0] - b[0]) * (0.5 / count)
+    return jnp.stack([total, spread])
+
+
+def pair_moments(stats, members):
+    core = lax.axis_index("grp") % 2
+    own = lax.dynamic_index_in_dim(stats, core, 0, keepdims=False)
+    other = lax.dynamic_index_in_dim(stats, 1 - core, 0, keepdims=False)
+    return join(own, swap(other, 1), members).astype(BF16)
+
+
+def ensemble_moments(held, members):
     groups = lax.axis_size("grp")
     core = lax.axis_index("grp") % 2
-
-    def swap(value, bit):
-        return lax.ppermute(value, "grp", [(g, g ^ bit) for g in range(groups)])
-
-    def join(a, b, count):
-        a, b = a.astype(F32), b.astype(F32)
-        total = a[0] + b[0]
-        spread = (a[1] + b[1]) + jnp.square(a[0] - b[0]) * (0.5 / count)
-        return jnp.stack([total, spread])
-
-    own = lax.dynamic_index_in_dim(stats, core, 0, keepdims=False)
-    other = lax.dynamic_index_in_dim(stats, 1 - core, 0, keepdims=False)
-    held = join(own, swap(other, 1), members)
     bit, count = 2, 2 * members
     while bit < groups:
-        held = held.astype(BF16)
-        held = join(held, swap(held, bit), count)
+        held = join(held.astype(BF16), swap(held.astype(BF16), bit), count)
         bit, count = 2 * bit, 2 * count
     scale = jnp.array([1.0 / count, 1.0 / (count - 1)], F32)
     held = (held * scale[:, None, None, None]).astype(BF16)
@@ -258,11 +263,17 @@
     sent = [
         analyse(grid_state, table_t, b, chunk, bands) for b in range(0, members, chunk)
     ]
-    basis = lax.all_to_all(legendre, "lat", split_axis=1, concat_axis=0, tiled=True)
+    groups = lax.axis_size("grp")
+    turned = legendre.transpose(1, 0, 2).reshape(bands, local_waves * lat_rows, wave_count)
+    share = local_waves * lat_rows // groups
+    own = lax.dynamic_slice_in_dim(turned, lax.axis_index("grp") * share, share, axis=1)
+    basis = lax.all_gather(exchange(own), "grp", axis=1, tiled=True)
+    basis = basis.reshape(bands, local_waves, lat_rows, wave_count).transpose(1, 0, 2, 3)
+    basis = basis.reshape(local_waves, bands * lat_rows, wave_count)
     zonal_ids = lax.axis_index("lat") * local_waves + jnp.arange(local_waves, dtype=jnp.int32)
     total_ids = jnp.arange(wave_count, dtype=jnp.int32)
     triangle = total_ids[None, :] >= zonal_ids[:, None]
-    basis = jnp.where(triangle[None], basis, jnp.zeros_like(basis)).transpose(1, 0, 2)
+    basis = jnp.where(triangle[:, None], basis, jnp.zeros_like(basis))
     flipped = basis.transpose(0, 2, 1)
     received = [exchange(s) for s in sent]
     banded = [spectral(r, basis, flipped, damping, parts) for r in received]
@@ -272,11 +283,13 @@
     moments = []
     for q in range(parts):
         fields = [exchange(g[q]) for g in banded]
+        if moments:
+            fields, moments[-1] = lax.optimization_barrier((fields, moments[-1]))
         new_state, stats = physics(
             fields, noise_field, table, first, input_bias[None], middle_weight,
             output_weight, q, new_state,
         )
-        moments.append(ensemble_moments(stats, members))
+        moments.append(ensemble_moments(pair_moments(stats, members), members))
     joined = [jnp.concatenate([low, high], axis=2) for low, high in moments]
     ens_mean = jnp.concatenate([j[0] for j in joined], axis=0).astype(F32)
     ens_var = jnp.concatenate([j[1] for j in joined], axis=0).astype(F32)

time: 434 us -> 405 us (0.933)
  blocking collectives: 81.9 us -> 8.58 us
  waiting for transfers between devices: 210 us -> 236 us
  starting transfers between devices: 26.6 us -> 36.6 us
  other arithmetic: 19.9 us -> 24.5 us
    all_to_all x2 -> x0, blocking collectives: 81.9 us -> none  [per_device(): lax.all_to_all(v, 'lat', split_axis=0, concat_axis=0, tiled=True)]
    all_to_all x4 -> x7, waiting for transfers between devices: 148 us -> 187 us  [per_device(): lax.all_to_all(v, 'lat', split_axis=0, concat_axis=0, tiled=True)]
    all_to_all x4 -> x7, starting transfers between devices: 15.5 us -> 33.3 us  [per_device(): lax.all_to_all(v, 'lat', split_axis=0, concat_axis=0, tiled=True)]
    all_to_all x1 -> x0, waiting for transfers between devices: 10.8 us -> none  [per_device(): lax.all_to_all(legendre, 'lat', split_axis=1, concat_axis=0, tiled=True)]
    all_gather x0 -> x1, blocking collectives: none -> 8.58 us  [per_device(): basis = lax.all_gather(exchange(own), 'grp', axis=1, tiled=True)]
    all_to_all x1 -> x0, starting transfers between devices: 7.31 us -> none  [per_device(): lax.all_to_all(legendre, 'lat', split_axis=1, concat_axis=0, tiled=True)]
    all_to_all x2 -> x0, local copies, waits for them, and re-layouts: 4.46 us -> none  [per_device(): lax.all_to_all(legendre, 'lat', split_axis=1, concat_axis=0, tiled=True)]
  transfers between devices with their start and end apart: 11 -> 13, of which waited for: 9 -> 12; matrix products, arithmetic and copies ran while one was open for 5% -> 6% of each run, Pallas kernels for 19% -> 15%
where the time goes in v2:
time: 405 us; the launch traced here: 403 us
  waiting for transfers between devices  236 us (58%)
  Pallas kernels  80.3 us (20%)
  starting transfers between devices  36.6 us (9%)
  other arithmetic  24.5 us (6%)
  local copies, waits for them, and re-layouts  15.9 us (4%)
  blocking collectives  8.58 us (2%)
    all_to_all x7, waiting for transfers between devices, per_device(): lax.all_to_all(v, 'lat', split_axis=0, concat_axis=0, tiled=True)  187 us
    ppermute x6, waiting for transfers between devices, swap(): return lax.ppermute(value, 'grp', [(g, g ^ bit) for g in range(groups)])  50 us
    pallas_call x2, Pallas kernels, physics(): pl.pallas_call(functools.partial(physics_body, len(fields)), grid=(part_r...  41.2 us
    all_to_all x7, starting transfers between devices, per_device(): lax.all_to_all(v, 'lat', split_axis=0, concat_axis=0, tiled=True)  33.3 us
    pallas_call x2, Pallas kernels, spectral(): pl.pallas_call(functools.partial(spectral_body, parts), grid=(count,), in...  23.7 us
    pallas_call x2, Pallas kernels, analyse(): pl.pallas_call(analysis_body, grid=(count, lat_rows // rows), in_specs=[p...  15.4 us
    all_gather x1, blocking collectives, per_device(): basis = lax.all_gather(exchange(own), 'grp', axis=1, tiled=True)  8.58 us
    unnamed x27, local copies, waits for them, and re-layouts  8.52 us
  transfers between devices with their start and end apart: 13, of which 12 were waited for; matrix products, arithmetic and copies ran while one was open for 6% of the time, Pallas kernels for 15%

profile of v2, /device:TPU:0, one launch (start us, length us, event | category | flops | bytes accessed | tf_op | source)
XLA Modules:
  0.0 403.4 jit_solution(1593279528309044017)
XLA Ops:
  0.6 1.6 copy.19
  2.3 0.7 constant_dynamic-slice_fusion
  3.0 7.3 %all-to-all-start.1 = ((bf16[8,96,128]{2,1,0:T(8,128)(2,1)}), bf16[8,96,128]{2,1,0:T(8,128)(2,1)S(1)}, u32[]{:S(2)}, u32[]{:S(2)}) async-start(bf16[8,96,128]{2,1,0:T(8,128)(2,1)} %constant_dynamic-slice_fusion), calls=%async_computation.1 | async-start | bytes 393216 | tf_op jit(solution)/shard_map/all_to_all | solution.py:260
  10.3 0.9 fusion.16
  11.2 0.7 fusion.11
  11.9 7.7 %shard_map.132 = bf16[8,2,24,32,128]{4,3,2,1,0:T(8,128)(2,1)} custom-call(bf16[256,384]{1,0:T(8,128)(2,1)} %bitcast.49, bf16[4,24,384,128]{3,2,1,0:T(8,128)(2,1)} %grid_ref.3), custom_call_target="tpu_custom_call" | custom-call | flops 1207959552 | bytes 9437184 | tf_op jit(solution)/shard_map/pallas_call | solution.py:45
  19.6 6.0 %all-to-all-start.3 = ((bf16[8,2,24,32,128]{4,3,2,1,0:T(8,128)(2,1)}), bf16[8,2,24,32,128]{4,3,2,1,0:T(8,128)(2,1)S(1)}, u32[]{:S(2)}, u32[]{:S(2)}) async-start(bf16[8,2,24,32,128]{4,3,2,1,0:T(8,128)(2,1)} %shard_map.132), calls=%async_computation.3 | async-start | bytes 6291456 | tf_op jit(solution)/shard_map/all_to_all | solution.py:260
  25.6 7.7 %shard_map.130 = bf16[8,2,24,32,128]{4,3,2,1,0:T(8,128)(2,1)} custom-call(bf16[256,384]{1,0:T(8,128)(2,1)} %bitcast.50, bf16[4,24,384,128]{3,2,1,0:T(8,128)(2,1)} %grid_ref.3), custom_call_target="tpu_custom_call" | custom-call | flops 1207959552 | bytes 9437184 | tf_op jit(solution)/shard_map/pallas_call | solution.py:45
  33.3 62.4 %all-to-all-done.3.in_ref = bf16[8,2,24,32,128]{4,3,2,1,0:T(8,128)(2,1)S(1)} async-done(((bf16[8,2,24,32,128]{4,3,2,1,0:T(8,128)(2,1)}), bf16[8,2,24,32,128]{4,3,2,1,0:T(8,128)(2,1)S(1)}, u32[]{:S(2)}, u32[]{:S(2)}) %all-to-all-start.3) | async-done | bytes 3145760 | tf_op jit(solution)/shard_map/all_to_all | solution.py:260
  95.8 1.7 copy-done.1
  97.4 3.7 all-to-all-start
  101.2 0.7 add_divide_fusion.damping_ref
  101.9 8.6 %all_gather.3 = bf16[8,384,128]{2,1,0:T(8,128)(2,1)S(1)} all-gather(bf16[8,96,128]{2,1,0:T(8,128)(2,1)S(1)} %all-to-all-done.1), channel_id=1, replica_groups=mesh['grp'=4,'lat'=8] {'grp'}, dimensions={1}, use_global_device_ids=true | all-gather | bytes 983040 | tf_op jit(solution)/shard_map/all_gather | solution.py:270
  110.5 1.0 copy.20
  111.5 2.2 copy.21
  113.7 2.3 broadcast_select_fusion.4
  116.0 2.2 copy.22.basis_ref
  118.2 2.3 fusion.22.flipped_ref
  120.5 11.8 %shard_map.133 = (bf16[8,2,12,32,128]{4,3,2,1,0:T(8,128)(2,1)}, bf16[8,2,12,32,128]{4,3,2,1,0:T(8,128)(2,1)}) custom-call(bf16[8,2,24,32,128]{4,3,2,1,0:T(8,128)(2,1)} %copy-done.1, bf16[16,192,128]{2,1,0:T(8,128)(2,1)} %copy.22.basis_ref, bf16[16,128,192]{2,1,0:T(8,128)(2,1)} %fusion.22.flipped_ref, f32[128,128]{1,0:T(8,128)} %add_divide_fusion.damping_ref), custom_call_target="tpu_custom_call" | custom-call | flops 805306368 | bytes 6291456 | tf_op jit(solution)/shard_map/pallas_call | solution.py:97
  132.3 39.6 %all-to-all-done.in_ref = bf16[8,2,24,32,128]{4,3,2,1,0:T(8,128)(2,1)S(1)} async-done(((bf16[8,2,24,32,128]{4,3,2,1,0:T(8,128)(2,1)}), bf16[8,2,24,32,128]{4,3,2,1,0:T(8,128)(2,1)S(1)}, u32[]{:S(2)}, u32[]{:S(2)}) %all-to-all-start) | async-done | bytes 3145760 | tf_op jit(solution)/shard_map/all_to_all | solution.py:260
  171.9 1.7 copy-done
  173.6 4.5 %all-to-all-start.6 = ((bf16[8,2,12,32,128]{4,3,2,1,0:T(8,128)(2,1)}), bf16[8,2,12,32,128]{4,3,2,1,0:T(8,128)(2,1)}, u32[]{:S(2)}, u32[]{:S(2)}) async-start(bf16[8,2,12,32,128]{4,3,2,1,0:T(8,128)(2,1)} %get-tuple-element.18), calls=%async_computation.6 | async-start | bytes 3145728 | tf_op jit(solution)/shard_map/all_to_all | solution.py:260
  178.1 11.9 %shard_map.131 = (bf16[8,2,12,32,128]{4,3,2,1,0:T(8,128)(2,1)}, bf16[8,2,12,32,128]{4,3,2,1,0:T(8,128)(2,1)}) custom-call(bf16[8,2,24,32,128]{4,3,2,1,0:T(8,128)(2,1)} %copy-done, bf16[16,192,128]{2,1,0:T(8,128)(2,1)} %copy.22.basis_ref, bf16[16,128,192]{2,1,0:T(8,128)(2,1)} %fusion.22.flipped_ref, f32[128,128]{1,0:T(8,128)} %add_divide_fusion.damping_ref), custom_call_target="tpu_custom_call" | custom-call | flops 805306368 | bytes 6291456 | tf_op jit(solution)/shard_map/pallas_call | solution.py:97
  190.0 24.7 %all-to-all-done.6.refs_1_ = bf16[8,2,12,32,128]{4,3,2,1,0:T(8,128)(2,1)} async-done(((bf16[8,2,12,32,128]{4,3,2,1,0:T(8,128)(2,1)}), bf16[8,2,12,32,128]{4,3,2,1,0:T(8,128)(2,1)}, u32[]{:S(2)}, u32[]{:S(2)}) %all-to-all-start.6) | async-done | bytes 1572896 | tf_op jit(solution)/shard_map/all_to_all | solution.py:260
  214.6 3.7 all-to-all-start.5
  218.4 0.8 copy.24.refs_3_
  219.3 36.2 %all-to-all-done.5.refs_0_ = bf16[8,2,12,32,128]{4,3,2,1,0:T(8,128)(2,1)S(1)} async-done(((bf16[8,2,12,32,128]{4,3,2,1,0:T(8,128)(2,1)}), bf16[8,2,12,32,128]{4,3,2,1,0:T(8,128)(2,1)S(1)}, u32[]{:S(2)}, u32[]{:S(2)}) %all-to-all-start.5) | async-done | bytes 1572896 | tf_op jit(solution)/shard_map/all_to_all | solution.py:260
  255.5 1.1 copy-done.6
  256.6 3.6 all-to-all-start.4
  260.3 20.5 %shard_map.134 = (bf16[4,24,384,128]{3,2,1,0:T(8,128)(2,1)}, bf16[2,2,12,192,128]{4,3,2,1,0:T(8,128)(2,1)}) custom-call(bf16[8,2,12,32,128]{4,3,2,1,0:T(8,128)(2,1)} %copy-done.6, bf16[8,2,12,32,128]{4,3,2,1,0:T(8,128)(2,1)} %all-to-all-done.6.refs_1_, bf16[4,24,384,128]{3,2,1,0:T(8,128)(2,1)} %refs_2_.3, bf16[384,256]{1,0:T(8,128)(2,1)} %copy.24.refs_3_, ...), custom_call_target="tpu_custom_call" | custom-call | flops 7247757312 | bytes 18874368 | tf_op jit(solution)/shard_map/pallas_call | solution.py:181
  280.7 1.9 dynamic-slice_convert_fusion.1
  282.7 2.8 collective-permute-done
  285.6 0.2 convert_element_type.68
  285.8 0.4 add_convert_fusion.1
  286.2 2.0 fusion.21
  288.2 1.5 collective-permute-start.1
  289.7 7.7 %all-to-all-done.4.refs_1_ = bf16[8,2,12,32,128]{4,3,2,1,0:T(8,128)(2,1)S(1)} async-done(((bf16[8,2,12,32,128]{4,3,2,1,0:T(8,128)(2,1)}), bf16[8,2,12,32,128]{4,3,2,1,0:T(8,128)(2,1)S(1)}, u32[]{:S(2)}, u32[]{:S(2)}) %all-to-all-start.4) | async-done | bytes 1572896 | tf_op jit(solution)/shard_map/all_to_all | solution.py:260
  297.5 1.1 copy-done.5
  298.6 4.5 %all-to-all-start.2 = ((bf16[8,2,12,32,128]{4,3,2,1,0:T(8,128)(2,1)}), bf16[8,2,12,32,128]{4,3,2,1,0:T(8,128)(2,1)}, u32[]{:S(2)}, u32[]{:S(2)}) async-start(bf16[8,2,12,32,128]{4,3,2,1,0:T(8,128)(2,1)} %get-tuple-element.15), calls=%async_computation.2 | async-start | bytes 3145728 | tf_op jit(solution)/shard_map/all_to_all | solution.py:260
  303.1 13.3 %collective-permute-done.1 = bf16[2,12,192,128]{3,2,1,0:T(8,128)(2,1)S(1)} collective-permute-done((bf16[2,12,192,128]{3,2,1,0:T(8,128)(2,1)}, bf16[2,12,192,128]{3,2,1,0:T(8,128)(2,1)S(1)}, u32[]{:S(2)}, u32[]{:S(2)}) %collective-permute-start.1) | collective-permute-done | bytes 1179680 | tf_op jit(solution)/shard_map/ppermute | solution.py:204
  316.5 0.2 convert_element_type.70
  316.7 0.3 slice_add_fusion.5
  317.1 0.3 copy-done.10
  317.4 0.3 fusion
  317.8 3.0 collective-permute-done.2
  320.8 3.1 broadcast_select_fusion.2
  323.8 15.8 %all-to-all-done.2.refs_0_ = bf16[8,2,12,32,128]{4,3,2,1,0:T(8,128)(2,1)} async-done(((bf16[8,2,12,32,128]{4,3,2,1,0:T(8,128)(2,1)}), bf16[8,2,12,32,128]{4,3,2,1,0:T(8,128)(2,1)}, u32[]{:S(2)}, u32[]{:S(2)}) %all-to-all-start.2) | async-done | bytes 1572896 | tf_op jit(solution)/shard_map/all_to_all | solution.py:260
  339.7 20.7 %shard_map.135 = (bf16[4,24,384,128]{3,2,1,0:T(8,128)(2,1)}, bf16[2,2,12,192,128]{4,3,2,1,0:T(8,128)(2,1)}) custom-call(bf16[8,2,12,32,128]{4,3,2,1,0:T(8,128)(2,1)} %all-to-all-done.2.refs_0_, bf16[8,2,12,32,128]{4,3,2,1,0:T(8,128)(2,1)} %copy-done.5, bf16[4,24,384,128]{3,2,1,0:T(8,128)(2,1)} %refs_2_.3, ...), custom_call_target="tpu_custom_call", output_to_operand_aliasing={{0}: (8, {})} | custom-call | flops 7247757312 | bytes 18874368 | tf_op jit(solution)/shard_map/pallas_call | solution.py:181
  360.4 1.9 dynamic-slice_convert_fusion
  362.4 2.8 collective-permute-done.3
  365.2 0.2 convert_element_type.73
  365.4 0.4 add_convert_fusion
  365.8 0.2 fusion.20
  366.1 1.6 collective-permute-start.4
  367.6 26.5 %collective-permute-done.4 = bf16[2,12,192,128]{3,2,1,0:T(8,128)(2,1)S(1)} collective-permute-done((bf16[2,12,192,128]{3,2,1,0:T(8,128)(2,1)S(1)}, bf16[2,12,192,128]{3,2,1,0:T(8,128)(2,1)S(1)}, u32[]{:S(2)}, u32[]{:S(2)}) %collective-permute-start.4) | collective-permute-done | bytes 1179680 | tf_op jit(solution)/shard_map/ppermute | solution.py:204
  394.2 0.2 convert_element_type.75
  394.4 0.4 slice_add_fusion.4
  394.9 0.4 fusion.1
  395.3 0.8 copy-done.3
  396.4 0.2 slice_bitcast_fusion
  396.6 1.5 collective-permute-done.5
  398.1 0.7 broadcast_select_fusion
  398.9 0.2 fusion.4
  399.1 4.3 %maximum_convert_fusion = (f32[24,384,128]{2,1,0:T(8,128)}, f32[24,384,128]{2,1,0:T(8,128)}) fusion(bf16[12,384,128]{2,1,0:T(8,128)(2,1)S(1)} %get-tuple-element.38, bf16[12,384,128]{2,1,0:T(8,128)(2,1)S(1)} %get-tuple-element.36, bf16[12,384,128]{2,1,0:T(8,128)(2,1)S(1)} %get-tuple-element.37, bf16[12,384,128]{2,1,0:T(8,128)(2,1)S(1)} %get-tuple-element.35), kind=kLoop, calls=%fused_computation.6 | loop fusion | flops 4718592 | bytes 14155776 | tf_op jit(solution)/shard_map/convert_element_type | solution.py:294
  (31 shorter events, 0.7 us)
Async XLA Ops:
  3.0 16.6 %all-to-all-start.1 = ((bf16[8,96,128]{2,1,0:T(8,128)(2,1)}), bf16[8,96,128]{2,1,0:T(8,128)(2,1)S(1)}, u32[]{:S(2)}, u32[]{:S(2)}) async-start(bf16[8,96,128]{2,1,0:T(8,128)(2,1)} %constant_dynamic-slice_fusion), calls=%async_computation.1 | async-start | bytes 393216 | tf_op jit(solution)/shard_map/all_to_all | solution.py:260
  19.6 76.1 %all-to-all-start.3 = ((bf16[8,2,24,32,128]{4,3,2,1,0:T(8,128)(2,1)}), bf16[8,2,24,32,128]{4,3,2,1,0:T(8,128)(2,1)S(1)}, u32[]{:S(2)}, u32[]{:S(2)}) async-start(bf16[8,2,24,32,128]{4,3,2,1,0:T(8,128)(2,1)} %shard_map.132), calls=%async_computation.3 | async-start | bytes 6291456 | tf_op jit(solution)/shard_map/all_to_all | solution.py:260
  33.3 67.9 %copy-start.11 = (f32[128]{0:T(128)S(1)}, f32[128]{0:T(128)}, u32[]{:S(2)}) copy-start(f32[128]{0:T(128)} %param.14) | copy-start | bytes 1540
  95.7 1.7 copy-start.1
  97.4 74.5 %all-to-all-start = ((bf16[8,2,24,32,128]{4,3,2,1,0:T(8,128)(2,1)}), bf16[8,2,24,32,128]{4,3,2,1,0:T(8,128)(2,1)S(1)}, u32[]{:S(2)}, u32[]{:S(2)}) async-start(bf16[8,2,24,32,128]{4,3,2,1,0:T(8,128)(2,1)} %shard_map.130), calls=%async_computation | async-start | bytes 6291456 | tf_op jit(solution)/shard_map/all_to_all | solution.py:260
  171.9 1.7 copy-start
  173.6 41.0 %all-to-all-start.6 = ((bf16[8,2,12,32,128]{4,3,2,1,0:T(8,128)(2,1)}), bf16[8,2,12,32,128]{4,3,2,1,0:T(8,128)(2,1)}, u32[]{:S(2)}, u32[]{:S(2)}) async-start(bf16[8,2,12,32,128]{4,3,2,1,0:T(8,128)(2,1)} %get-tuple-element.18), calls=%async_computation.6 | async-start | bytes 3145728 | tf_op jit(solution)/shard_map/all_to_all | solution.py:260
  214.6 3.7 copy-start.4
  214.6 4.6 %copy-start.7 = (bf16[128,256]{1,0:T(8,128)(2,1)S(1)}, bf16[128,256]{1,0:T(8,128)(2,1)}, u32[]{:S(2)}) copy-start(bf16[128,256]{1,0:T(8,128)(2,1)} %param.15) | copy-start | bytes 196612
  214.6 4.6 %copy-start.8 = (bf16[128,256]{1,0:T(8,128)(2,1)S(1)}, bf16[128,256]{1,0:T(8,128)(2,1)}, u32[]{:S(2)}) copy-start(bf16[128,256]{1,0:T(8,128)(2,1)} %param.16) | copy-start | bytes 196612
  214.6 40.9 %all-to-all-start.5 = ((bf16[8,2,12,32,128]{4,3,2,1,0:T(8,128)(2,1)}), bf16[8,2,12,32,128]{4,3,2,1,0:T(8,128)(2,1)S(1)}, u32[]{:S(2)}, u32[]{:S(2)}) async-start(bf16[8,2,12,32,128]{4,3,2,1,0:T(8,128)(2,1)} %get-tuple-element.17), calls=%async_computation.5 | async-start | bytes 3145728 | tf_op jit(solution)/shard_map/all_to_all | solution.py:260
  219.3 36.2 %copy-start.9 = (bf16[256,256]{1,0:T(8,128)(2,1)}, bf16[256,256]{1,0:T(8,128)(2,1)S(1)}, u32[]{:S(2)}) copy-start(bf16[256,256]{1,0:T(8,128)(2,1)S(1)} %constant_dynamic-update-slice_fusion.refs_4_) | copy-start | bytes 393220
  255.5 1.1 copy-start.6
  256.6 40.8 %all-to-all-start.4 = ((bf16[8,2,12,32,128]{4,3,2,1,0:T(8,128)(2,1)}), bf16[8,2,12,32,128]{4,3,2,1,0:T(8,128)(2,1)S(1)}, u32[]{:S(2)}, u32[]{:S(2)}) async-start(bf16[8,2,12,32,128]{4,3,2,1,0:T(8,128)(2,1)} %get-tuple-element.16), calls=%async_computation.4 | async-start | bytes 3145728 | tf_op jit(solution)/shard_map/all_to_all | solution.py:260
  282.6 2.9 collective-permute-start
  288.2 28.2 %collective-permute-start.1 = (bf16[2,12,192,128]{3,2,1,0:T(8,128)(2,1)}, bf16[2,12,192,128]{3,2,1,0:T(8,128)(2,1)S(1)}, u32[]{:S(2)}, u32[]{:S(2)}) collective-permute-start(bf16[2,12,192,128]{3,2,1,0:T(8,128)(2,1)} %get-tuple-element.50), channel_id=1, source_target_pairs={{0,16},{8,24},{16,0},{24,8},{1,17},{9,25},{17,1},{25,9},{2,18},{10... | collective-permute-start | bytes 3538952 | tf_op jit(solution)/shard_map/ppermute | solution.py:204
  297.5 1.1 copy-start.5
  298.6 41.0 %all-to-all-start.2 = ((bf16[8,2,12,32,128]{4,3,2,1,0:T(8,128)(2,1)}), bf16[8,2,12,32,128]{4,3,2,1,0:T(8,128)(2,1)}, u32[]{:S(2)}, u32[]{:S(2)}) async-start(bf16[8,2,12,32,128]{4,3,2,1,0:T(8,128)(2,1)} %get-tuple-element.15), calls=%async_computation.2 | async-start | bytes 3145728 | tf_op jit(solution)/shard_map/all_to_all | solution.py:260
  303.1 13.6 %copy-start.2 = (f32[2,12,192,128]{3,2,1,0:T(8,128)S(1)}, f32[2,12,192,128]{3,2,1,0:T(8,128)}, u32[]{:S(2)}) copy-start(f32[2,12,192,128]{3,2,1,0:T(8,128)} %get-tuple-element.49) | copy-start | bytes 7077892
  316.7 0.7 copy-start.10
  317.7 3.0 collective-permute-start.2
  362.3 2.9 collective-permute-start.3
  366.1 28.1 %collective-permute-start.4 = (bf16[2,12,192,128]{3,2,1,0:T(8,128)(2,1)S(1)}, bf16[2,12,192,128]{3,2,1,0:T(8,128)(2,1)S(1)}, u32[]{:S(2)}, u32[]{:S(2)}) collective-permute-start(bf16[2,12,192,128]{3,2,1,0:T(8,128)(2,1)S(1)} %get-tuple-element.48), channel_id=1, source_target_pairs={{0,16},{8,24},{16,0},{24,8},{1,17},{9,25},{17,1},{25,9},{2,18},{10... | collective-permute-start | bytes 3538952 | tf_op jit(solution)/shard_map/ppermute | solution.py:204
  394.9 1.3 copy-start.3
  395.2 2.9 collective-permute-start.5
